TPU v7x, 32 devices: a whole 2x2x4 slice. The times are simulated.
32 devices in a mesh: pts: 8 (over z, core), head: 4 (over y, x).
Axes of the slice: x: 2, y: 2, z: 4, core: 2. Of those that a mesh axis runs over, the one named last changes fastest.
Arguments:
- points: bfloat16 [73728, 128], P('pts')
- counts: int32 [8], P('pts'), may hold values from 1 to 9216, 55296 in all
- ln1_gain: float32 [2, 128], replicated, may hold values from 0.5 to 1.5
- ln1_bias: float32 [2, 128], replicated, may hold values from -1.5 to 1.5
- w_in: bfloat16 [2, 128, 128], P(None, None, 'head'), may hold values from -0.5 to 0.5
- w_fx: bfloat16 [2, 128, 128], P(None, None, 'head'), may hold values from -0.5 to 0.5
- w_slice: bfloat16 [2, 32, 32], replicated
- temper: float32 [2, 4], replicated, may hold values from 0.5 to 2
- query_weight: bfloat16 [2, 32, 32], replicated
- key_weight: bfloat16 [2, 32, 32], replicated, may hold values from -1 to 1
- value_weight: bfloat16 [2, 32, 32], replicated, may hold values from -1 to 1
- w_out: bfloat16 [2, 128, 128], P(None, 'head'), may hold values from -1 to 1
- b_out: float32 [2, 128], replicated, may hold values from -1.5 to 1.5
- ln2_gain: float32 [2, 128], replicated, may hold values from 0.5 to 1.5
- ln2_bias: float32 [2, 128], replicated, may hold values from -1.5 to 1.5
- w_up: bfloat16 [2, 128, 512], replicated, may hold values from -0.5 to 0.5
- w_down: bfloat16 [2, 512, 128], replicated, may hold values from -0.25 to 0.25
Outputs:
- features: bfloat16 [73728, 128], P(('pts', 'head'))
Inputs may be any that keep to these rules, and one draw needn't show every extreme that they name: counts[i] live points fill the first slots of shard i; at least one shard is full; they sum to 55296.
All inputs are finite; a program needn't handle non-finite values.
Results may differ from a plain program's by a relative error of at most 0.014.
Values may be sent and summed in bfloat16 or wider, within the bound.
A program may use at most 128 MiB of HBM per device.

v0:
```python
import jax
import jax.numpy as jnp
from jax import lax
from jax.sharding import PartitionSpec as P

DH = 32
M = 32


def layer_norm(value, gain, bias):
    mean = jnp.mean(value, axis=-1, keepdims=True)
    centred = value - mean
    var = jnp.mean(centred * centred, axis=-1, keepdims=True)
    return centred * lax.rsqrt(var + 1e-05) * gain + bias


def slice_attention(token_rows, query_weight, key_weight, value_weight):
    head_parts = lax.Precision.HIGHEST
    query_rows = jnp.einsum(
        "aur,rz->auz", token_rows, query_weight.astype(jnp.float32), precision=head_parts
    )
    slice_keys = jnp.einsum(
        "aur,rz->auz", token_rows, key_weight.astype(jnp.float32), precision=head_parts
    )
    slice_values = jnp.einsum(
        "aur,rz->auz", token_rows, value_weight.astype(jnp.float32), precision=head_parts
    )
    scores = jnp.einsum("hme,hke->hmk", query_rows, slice_keys, precision=head_parts) * DH ** (-0.5)
    attn = jax.nn.softmax(scores, axis=-1)
    return jnp.einsum("hmk,hke->hme", attn, slice_values, precision=head_parts).astype(jnp.bfloat16)


def body(
    points,
    counts,
    ln1_gain,
    ln1_bias,
    w_in,
    w_fx,
    w_slice,
    temper,
    query_weight,
    key_weight,
    value_weight,
    w_out,
    b_out,
    ln2_gain,
    ln2_bias,
    w_up,
    w_down,
):
    groups = lax.axis_size("head")
    rows = points.shape[0] // groups
    first_row = lax.axis_index("head") * rows
    layers = w_in.shape[0]
    full_in = lax.all_gather(w_in, "head", axis=2, tiled=True)
    full_fx = lax.all_gather(w_fx, "head", axis=2, tiled=True)
    full_out = lax.all_gather(w_out, "head", axis=1, tiled=True)
    heads = full_in.shape[2] // DH
    live = (first_row + jnp.arange(rows, dtype=jnp.int32) < counts[0]).astype(jnp.float32)
    current = lax.dynamic_slice_in_dim(points, first_row, rows, 0)
    for layer_index in range(layers):
        normed = layer_norm(
            current.astype(jnp.float32), ln1_gain[layer_index], ln1_bias[layer_index]
        ).astype(jnp.bfloat16)
        mid = jnp.dot(normed, full_in[layer_index], preferred_element_type=jnp.float32).astype(
            jnp.bfloat16
        )
        feats = jnp.dot(normed, full_fx[layer_index], preferred_element_type=jnp.float32).astype(
            jnp.bfloat16
        )
        spread = jnp.kron(jnp.eye(heads, dtype=jnp.bfloat16), w_slice[layer_index])
        logits = jnp.dot(mid, spread, preferred_element_type=jnp.float32)
        logits = logits.reshape(rows, heads, M) / temper[layer_index][None, :, None]
        weights = jax.nn.softmax(logits, axis=-1) * live[:, None, None]
        half_weights = weights.astype(jnp.bfloat16).reshape(rows, heads * M)
        total = jnp.sum(weights, axis=0)
        square = jnp.einsum("rs,rl->sl", half_weights, feats, preferred_element_type=jnp.float32)
        square = square.reshape(heads, M, heads, DH)
        numerator = jnp.stack([square[h, :, h, :] for h in range(heads)])
        numerator, total = lax.psum((numerator, total), ("pts", "head"))
        token_rows = numerator / jnp.maximum(total, 1.0)[..., None]
        mixed_token = slice_attention(
            token_rows,
            query_weight[layer_index],
            key_weight[layer_index],
            value_weight[layer_index],
        )
        wide = (
            jnp.einsum(
                "hmv,hvc->hmc",
                mixed_token,
                full_out[layer_index].reshape(heads, DH, -1),
                preferred_element_type=jnp.float32,
            )
            .astype(jnp.bfloat16)
            .reshape(heads * M, -1)
        )
        projected = jnp.dot(half_weights, wide, preferred_element_type=jnp.float32)
        after = current.astype(jnp.float32) + projected + b_out[layer_index]
        normed2 = layer_norm(after, ln2_gain[layer_index], ln2_bias[layer_index]).astype(
            jnp.bfloat16
        )
        upper = jax.nn.gelu(
            jnp.dot(normed2, w_up[layer_index], preferred_element_type=jnp.float32)
        ).astype(jnp.bfloat16)
        current = (
            after + jnp.dot(upper, w_down[layer_index], preferred_element_type=jnp.float32)
        ).astype(jnp.bfloat16)
    return current


def solution(mesh):
    placed = (
        P("pts", None),
        P("pts"),
        P(),
        P(),
        P(None, None, "head"),
        P(None, None, "head"),
        P(),
        P(),
        P(),
        P(),
        P(),
        P(None, "head", None),
        P(),
        P(),
        P(),
        P(),
        P(),
    )
    return jax.shard_map(
        body, mesh=mesh, in_specs=placed, out_specs=P(("pts", "head"), None), check_vma=False
    )
```

profile of v0, /device:TPU:0, one launch (start us, length us, event | category | flops | bytes accessed | tf_op | source)
XLA Modules:
  0.0 157.5 jit_solution(5383199505180625222)
XLA Ops:
  0.0 1.7 %copy-done = bf16[9216,128]{1,0:T(8,128)(2,1)S(1)} copy-done((bf16[9216,128]{1,0:T(8,128)(2,1)S(1)}, bf16[9216,128]{1,0:T(8,128)(2,1)}, u32[]{:S(2)}) %copy-start) | copy-done | bytes 2359320
  1.7 0.0 copy-start.13
  1.7 0.2 copy.26
  2.0 0.0 copy-start.18
  2.0 0.0 copy-start.19
  2.0 0.0 copy-start.10
  2.0 0.0 copy-start.16
  2.0 0.1 convert_reduce_fusion
  2.1 0.2 fusion.33
  2.3 0.3 copy-done.18
  2.7 0.0 copy-done.19
  2.7 0.6 slice_bitcast_fusion.34
  3.3 0.1 copy.19
  3.4 0.1 copy.20
  3.5 0.8 broadcast_multiply_fusion
  4.3 0.1 mul.187
  4.4 9.7 %all_gather.9 = bf16[2,128,128]{1,2,0:T(8,128)(2,1)S(1)} all-gather(bf16[2,128,32]{1,2,0:T(8,128)(2,1)S(1)} %copy-done.10), channel_id=1, replica_groups=mesh['pts'=8,'head'=4] {'head'}, dimensions={2}, use_global_device_ids=true | all-gather | bytes 81920 | tf_op jit(solution)/shard_map/all_gather | solution.py:56
  14.2 1.9 %fusion.122 = (f32[2304,4]{0,1:T(4,128)S(1)}, f32[2304,4,32]{0,2,1:T(8,128)}) fusion(bf16[4,32,128]{2,1,0:T(8,128)(2,1)S(1)} %bitcast.209, f32[4]{0:T(128)S(1)} %get-tuple-element.28, bf16[2,128,128]{1,2,0:T(8,128)(2,1)S(1)} %all_gather.9, bf16[2304,128]{0,1:T(8,128)(2,1)S(1)} %copy.26, f32[128]{0:T(128)S(1)} %get-tuple-element.34, ...), kind=kOutput, calls=%fused_computation.175 | convolution fusion | flops 153944096 | bytes 1897984 | tf_op jit(solution)/shard_map/sub | solution.py:75
  16.0 0.0 copy-start.11
  16.7 1.6 %fusion.57 = f32[4,32]{1,0:T(4,128)S(1)} fusion(f32[2304]{0:T(1024)S(1)} %fusion.83, f32[2304,4,32]{0,2,1:T(8,128)} %get-tuple-element.36, f32[2304,4]{0,1:T(4,128)S(1)} %get-tuple-element.35), kind=kLoop, calls=%fused_computation.77 | loop fusion | flops 884608 | bytes 1226240 | tf_op jit(solution)/shard_map/reduce_sum | solution.py:77
  18.3 8.2 %all_gather.10 = bf16[2,128,128]{1,2,0:T(8,128)(2,1)S(1)} all-gather(bf16[2,128,32]{1,2,0:T(8,128)(2,1)S(1)} %copy-done.11), channel_id=1, replica_groups=mesh['pts'=8,'head'=4] {'head'}, dimensions={2}, use_global_device_ids=true | all-gather | bytes 81920 | tf_op jit(solution)/shard_map/all_gather | solution.py:57
  26.5 0.4 convolution_convert_fusion.1
  27.0 0.0 copy-start.23
  27.0 0.0 copy-start.24
  27.0 0.0 copy-start.25
  27.0 0.6 fusion.39
  27.6 0.0 copy-start.12
  27.6 0.0 copy-start.17
  27.7 40.2 %all-reduce.1 = (f32[4,32,32]{2,1,0:T(8,128)S(1)}, f32[4,32]{1,0:T(4,128)S(1)}) all-reduce(f32[4,32,32]{2,1,0:T(8,128)S(1)} %pad_maximum_fusion, f32[4,32]{1,0:T(4,128)S(1)} %fusion.57), channel_id=1, replica_groups=mesh['pts'=8,'head'=4] {'pts','head'}, use_global_device_ids=true, to_apply=%region_4.5 | all-reduce | flops 4224 | bytes 33792 | tf_op jit(solution)/shard_map/psum | solution.py:81
  67.9 0.2 fusion.92
  68.2 0.2 fusion.94
  68.4 0.2 fusion.125
  68.7 0.2 fusion.90
  69.0 0.3 convolution_convert_fusion.7
  69.3 9.0 %all_gather.11 = bf16[2,128,128]{2,1,0:T(8,128)(2,1)S(1)} all-gather(bf16[2,32,128]{2,1,0:T(8,128)(2,1)S(1)} %copy-done.12), channel_id=1, replica_groups=mesh['pts'=8,'head'=4] {'head'}, dimensions={1}, use_global_device_ids=true | all-gather | bytes 81920 | tf_op jit(solution)/shard_map/all_gather | solution.py:58
  78.3 0.6 fusion.121
  78.9 0.5 slice_bitcast_fusion.32
  79.4 2.8 %fusion.126 = (f32[2304]{0:T(1024)S(1)}, f32[2304,128]{0,1:T(8,128)}) fusion(f32[128]{0:T(128)S(1)} %get-tuple-element.26, bf16[4,32,32]{2,1,0:T(8,128)(2,1)S(1)} %convolution_convert_fusion.7, bf16[4,32,128]{2,1,0:T(8,128)(2,1)S(1)} %bitcast.212, f32[2304]{0:T(1024)S(1)} %fusion.83, f32[2304,4,32]{0,2,1:T(8,128)} %get-tuple-element.36, ...), kind=kOutput, calls=%fused_computation.177 | convolution fusion | flops 78624512 | bytes 3045888 | tf_op jit(solution)/shard_map/dot_general | solution.py:99
  82.2 1.4 multiply_reduce_fusion.2
  83.6 0.6 add_rsqrt_fusion.2
  84.2 0.6 slice_bitcast_fusion.30
  84.8 4.6 %fusion.127 = (f32[2304]{0:T(1024)}, f32[2304,128]{0,1:T(8,128)S(1)}) fusion(f32[2304,128]{0,1:T(8,128)} %get-tuple-element.40, bf16[2,512,128]{2,1,0:T(8,128)(2,1)} %param.33, f32[128]{0:T(128)} %get-tuple-element.24, f32[128]{0:T(128)} %get-tuple-element.51, f32[2304]{0:T(1024)} %add_rsqrt_fusion.2, f32[2304]{0:T(1024)} %copy-done.8, ...), kind=kOutput, calls=%fused_computation.178 | convolution fusion | flops 617248512 | bytes 3835904 | tf_op jit(solution)/shard_map/dot_general | solution.py:108
  89.4 0.7 broadcast_multiply_fusion.3
  90.1 0.1 multiply_reduce_fusion.1
  90.3 1.2 add_convert_fusion.1
  91.5 1.6 %mul.210 = bf16[128,128]{0,1:T(8,128)(2,1)} reshape(bf16[4,32,4,32]{1,0,3,2:T(4,128)(2,1)} %get-tuple-element.29) | data formatting | bytes 65536 | tf_op jit(solution)/shard_map/jit(kron)/mul | solution.py:72
  93.1 3.4 %fusion.130 = (f32[2304,4]{0,1:T(4,128)}, f32[2304,4,32]{0,2,1:T(8,128)}) fusion(bf16[4,32,128]{2,1,0:T(8,128)(2,1)} %bitcast.210, bf16[2304,128]{0,1:T(8,128)(2,1)} %add_convert_fusion.1, f32[4]{0:T(128)S(1)} %get-tuple-element.27, bf16[2,128,128]{1,2,0:T(8,128)(2,1)} %copy-done.7), kind=kOutput, calls=%fused_computation.179 | convolution fusion | flops 152174624 | bytes 1871888 | tf_op jit(solution)/shard_map/sub | solution.py:75
  96.5 1.6 %fusion.59 = f32[4,32]{1,0:T(4,128)S(1)} fusion(f32[2304]{0:T(1024)S(1)} %fusion.83, f32[2304,4,32]{0,2,1:T(8,128)} %get-tuple-element.44, f32[2304,4]{0,1:T(4,128)} %get-tuple-element.43), kind=kLoop, calls=%fused_computation.79 | loop fusion | flops 884608 | bytes 1226240 | tf_op jit(solution)/shard_map/reduce_sum | solution.py:77
  98.2 0.3 convolution_convert_fusion
  98.5 0.6 fusion.37
  99.1 0.6 pad_maximum_fusion.1
  99.7 40.3 %all-reduce = (f32[4,32,32]{2,1,0:T(8,128)}, f32[4,32]{1,0:T(4,128)}) all-reduce(f32[4,32,32]{2,1,0:T(8,128)} %pad_maximum_fusion.1, f32[4,32]{1,0:T(4,128)S(1)} %fusion.59), channel_id=1, replica_groups=mesh['pts'=8,'head'=4] {'pts','head'}, use_global_device_ids=true, to_apply=%region_15.16 | all-reduce | flops 4224 | bytes 33792 | tf_op jit(solution)/shard_map/psum | solution.py:81
  140.0 0.7 broadcast_maximum_fusion
  140.7 1.1 fusion.86
  141.8 1.1 fusion.88
  142.9 0.2 fusion.131
  143.1 1.1 fusion.84
  144.2 0.9 convolution_convert_fusion.5
  145.2 3.4 %fusion.132 = (f32[2304]{0:T(1024)}, f32[2304,128]{0,1:T(8,128)}) fusion(f32[128]{0:T(128)} %get-tuple-element.25, f32[2304,128]{0,1:T(8,128)S(1)} %get-tuple-element.42, bf16[4,32,32]{2,1,0:T(8,128)(2,1)} %convolution_convert_fusion.5, bf16[4,32,128]{2,1,0:T(8,128)(2,1)} %bitcast.211, f32[2304]{0:T(1024)S(1)} %fusion.83, ...), kind=kOutput, calls=%fused_computation.181 | convolution fusion | flops 78329600 | bytes 3635712 | tf_op jit(solution)/shard_map/dot_general | solution.py:99
  148.6 0.8 broadcast_multiply_fusion.2
  149.4 1.4 multiply_reduce_fusion
  150.8 0.6 add_rsqrt_fusion
  151.4 4.0 %fusion.27 = bf16[2304,128]{0,1:T(8,128)(2,1)} fusion(f32[2304,128]{0,1:T(8,128)S(1)} %copy-done.4, f32[128]{0:T(128)S(1)} %copy-done.22, f32[128]{0:T(128)} %get-tuple-element.52, f32[2304]{0:T(1024)} %add_rsqrt_fusion, f32[2304]{0:T(1024)S(1)} %broadcast_multiply_fusion.2, bf16[2,512,128]{2,1,0:T(8,128)(2,1)} %param.33, bf16[2,128,512]{2,1,0:T(8,128)(2,1)} %param.32), kind=kOutput, calls=%fused_computation.35 | convolution fusion | flops 616660992 | bytes 3236864 | tf_op jit(solution)/shard_map/dot_general | solution.py:108
  155.4 2.1 %copy.22 = bf16[2304,128]{1,0:T(8,128)(2,1)} copy(bf16[2304,128]{0,1:T(8,128)(2,1)} %fusion.27) | data formatting | bytes 1179648 | tf_op jit(solution)/shard_map/convert_element_type | solution.py:109
  (53 shorter events, 0.3 us)
Async XLA Ops:
  0.0 1.7 %copy-start = (bf16[9216,128]{1,0:T(8,128)(2,1)S(1)}, bf16[9216,128]{1,0:T(8,128)(2,1)}, u32[]{:S(2)}) copy-start(bf16[9216,128]{1,0:T(8,128)(2,1)} %param.17) | copy-start | bytes 7077892
  1.7 1.6 copy-start.13
  2.0 0.7 copy-start.18
  2.0 0.7 copy-start.19
  2.0 2.4 %copy-start.10 = (bf16[2,128,32]{1,2,0:T(8,128)(2,1)S(1)}, bf16[2,128,32]{1,2,0:T(8,128)(2,1)}, u32[]{:S(2)}) copy-start(bf16[2,128,32]{1,2,0:T(8,128)(2,1)} %param.21) | copy-start | bytes 49156
  2.0 12.1 %copy-start.16 = (f32[2,4]{1,0:T(2,128)S(1)}, f32[2,4]{1,0:T(2,128)}, u32[]{:S(2)}) copy-start(f32[2,4]{1,0:T(2,128)} %param.24) | copy-start | bytes 100
  14.1 1.9 %copy-start.7 = (bf16[2,128,128]{1,2,0:T(8,128)(2,1)}, bf16[2,128,128]{1,2,0:T(8,128)(2,1)S(1)}, u32[]{:S(2)}) copy-start(bf16[2,128,128]{1,2,0:T(8,128)(2,1)S(1)} %all_gather.9) | copy-start | bytes 196612
  16.0 2.3 %copy-start.11 = (bf16[2,128,32]{1,2,0:T(8,128)(2,1)S(1)}, bf16[2,128,32]{1,2,0:T(8,128)(2,1)}, u32[]{:S(2)}) copy-start(bf16[2,128,32]{1,2,0:T(8,128)(2,1)} %param.22) | copy-start | bytes 49156
  16.7 10.3 %copy-start.2 = (f32[2304,4,32]{0,2,1:T(8,128)S(1)}, f32[2304,4,32]{0,2,1:T(8,128)}, u32[]{:S(2)}) copy-start(f32[2304,4,32]{0,2,1:T(8,128)} %get-tuple-element.36) | copy-start | bytes 3538948
  26.5 1.1 copy-start.5
  27.0 40.9 %copy-start.23 = (bf16[2,32,32]{2,1,0:T(8,128)(2,1)S(1)}, bf16[2,32,32]{2,1,0:T(8,128)(2,1)}, u32[]{:S(2)}) copy-start(bf16[2,32,32]{2,1,0:T(8,128)(2,1)} %param.26) | copy-start | bytes 12292
  27.0 41.2 %copy-start.24 = (bf16[2,32,32]{2,1,0:T(8,128)(2,1)S(1)}, bf16[2,32,32]{2,1,0:T(8,128)(2,1)}, u32[]{:S(2)}) copy-start(bf16[2,32,32]{2,1,0:T(8,128)(2,1)} %param.25) | copy-start | bytes 12292
  27.0 41.7 %copy-start.25 = (bf16[2,32,32]{2,1,0:T(8,128)(2,1)S(1)}, bf16[2,32,32]{2,1,0:T(8,128)(2,1)}, u32[]{:S(2)}) copy-start(bf16[2,32,32]{2,1,0:T(8,128)(2,1)} %param.27) | copy-start | bytes 12292
  27.6 41.6 %copy-start.12 = (bf16[2,32,128]{2,1,0:T(8,128)(2,1)S(1)}, bf16[2,32,128]{2,1,0:T(8,128)(2,1)}, u32[]{:S(2)}) copy-start(bf16[2,32,128]{2,1,0:T(8,128)(2,1)} %param.28) | copy-start | bytes 49156
  27.6 51.2 %copy-start.17 = (f32[2,128]{1,0:T(2,128)S(1)}, f32[2,128]{1,0:T(2,128)}, u32[]{:S(2)}) copy-start(f32[2,128]{1,0:T(2,128)} %param.29) | copy-start | bytes 3076
  82.2 2.1 %copy-start.20 = (f32[2,128]{1,0:T(2,128)S(1)}, f32[2,128]{1,0:T(2,128)}, u32[]{:S(2)}) copy-start(f32[2,128]{1,0:T(2,128)} %param.31) | copy-start | bytes 3076
  82.2 2.1 %copy-start.21 = (f32[2,128]{1,0:T(2,128)S(1)}, f32[2,128]{1,0:T(2,128)}, u32[]{:S(2)}) copy-start(f32[2,128]{1,0:T(2,128)} %param.30) | copy-start | bytes 3076
  82.2 2.7 %copy-start.8 = (f32[2304]{0:T(1024)}, f32[2304]{0:T(1024)S(1)}, u32[]{:S(2)}) copy-start(f32[2304]{0:T(1024)S(1)} %broadcast_multiply_fusion.4) | copy-start | bytes 27652
  89.4 0.9 copy-start.14
  89.4 0.9 copy-start.15
  96.5 1.6 %copy-start.1 = (bf16[2304,128]{0,1:T(8,128)(2,1)S(1)}, bf16[2304,128]{0,1:T(8,128)(2,1)}, u32[]{:S(2)}) copy-start(bf16[2304,128]{0,1:T(8,128)(2,1)} %add_convert_fusion.1) | copy-start | bytes 1769476
  96.5 1.6 %copy-start.6 = (bf16[2,128,128]{1,2,0:T(8,128)(2,1)S(1)}, bf16[2,128,128]{1,2,0:T(8,128)(2,1)}, u32[]{:S(2)}) copy-start(bf16[2,128,128]{1,2,0:T(8,128)(2,1)} %copy-done.5) | copy-start | bytes 196612
  96.5 2.0 %copy-start.3 = (f32[2304,4,32]{0,2,1:T(8,128)S(1)}, f32[2304,4,32]{0,2,1:T(8,128)}, u32[]{:S(2)}) copy-start(f32[2304,4,32]{0,2,1:T(8,128)} %get-tuple-element.44) | copy-start | bytes 3538948
  96.5 2.0 %copy-start.9 = (f32[2304,4]{0,1:T(4,128)S(1)}, f32[2304,4]{0,1:T(4,128)}, u32[]{:S(2)}) copy-start(f32[2304,4]{0,1:T(4,128)} %get-tuple-element.43) | copy-start | bytes 110596
  148.6 2.8 %copy-start.4 = (f32[2304,128]{0,1:T(8,128)S(1)}, f32[2304,128]{0,1:T(8,128)}, u32[]{:S(2)}) copy-start(f32[2304,128]{0,1:T(8,128)} %get-tuple-element.48) | copy-start | bytes 3538948
  148.6 2.8 %copy-start.22 = (f32[128]{0:T(128)S(1)}, f32[128]{0:T(128)}, u32[]{:S(2)}) copy-start(f32[128]{0:T(128)} %get-tuple-element.23) | copy-start | bytes 1540
where the time goes:
time: 159 us; the launch traced here: 158 us
  blocking collectives  107 us (67%)
  matrix products  27.6 us (17%)
  other arithmetic  12.6 us (8%)
  local copies, waits for them, and re-layouts  8.79 us (6%)
    psum x2, blocking collectives, body(): numerator, total = lax.psum((numerator, total), ('pts', 'head'))  80.5 us
    all_gather x1, blocking collectives, body(): full_in = lax.all_gather(w_in, 'head', axis=2, tiled=True)  9.72 us
    all_gather x1, blocking collectives, body(): full_out = lax.all_gather(w_out, 'head', axis=1, tiled=True)  9 us
    dot_general x2, matrix products, body(): jnp.dot(upper, w_down[layer_index], preferred_element_type=jnp.float32)  8.51 us
    all_gather x1, blocking collectives, body(): full_fx = lax.all_gather(w_fx, 'head', axis=2, tiled=True)  8.21 us
    dot_general x2, matrix products, body(): projected = jnp.dot(half_weights, wide, preferred_element_type=jnp.float32)  6.22 us
    sub x2, matrix products, body(): weights = jax.nn.softmax(logits, axis=-1) * live[:, None, None]  5.29 us
    reduce_sum x2, other arithmetic, body(): total = jnp.sum(weights, axis=0)  3.22 us

commit v1 on v0

--- a/solution.py
+++ b/solution.py
@@ -55,7 +55,24 @@
     layers = w_in.shape[0]
     full_in = lax.all_gather(w_in, "head", axis=2, tiled=True)
     full_fx = lax.all_gather(w_fx, "head", axis=2, tiled=True)
-    full_out = lax.all_gather(w_out, "head", axis=1, tiled=True)
+
+    def balance_page(message, out_dim):
+        shard_axis = "head"
+        entries = []
+        width = lax.axis_size(shard_axis)
+        for u in range(1, width):
+            entries.append((u - 1, u))
+        outcome_arr = message
+        x_new = entries + [(width - 1, 0)]
+        items = [outcome_arr]
+        for _ in range(width - 1):
+            outcome_arr = lax.ppermute(outcome_arr, axis_name=shard_axis, perm=x_new)
+            items += [outcome_arr]
+        v1 = jnp.concatenate([*reversed(items)], out_dim)
+        reply = lax.axis_index(shard_axis)
+        return jnp.roll(v1, (reply + 1) * outcome_arr.shape[out_dim], out_dim)
+
+    full_out = balance_page(w_out, 1)
     heads = full_in.shape[2] // DH
     live = (first_row + jnp.arange(rows, dtype=jnp.int32) < counts[0]).astype(jnp.float32)
     current = lax.dynamic_slice_in_dim(points, first_row, rows, 0)

time: 159 us -> 164 us (1.031)
  blocking collectives: 107 us -> 96.9 us
  starting transfers between devices: 0 us -> 6.71 us
  matrix products: 27.6 us -> 33.5 us
  waiting for transfers between devices: 0 us -> 3.96 us
    all_gather x1 -> x0, blocking collectives: 9 us -> none  [body(): full_out = lax.all_gather(w_out, 'head', axis=1, tiled=True)]
    ppermute x0 -> x3, starting transfers between devices: none -> 6.71 us  [balance_page(): outcome_arr = lax.ppermute(outcome_arr, axis_name=shard_axis, perm=x_new)]
    ppermute x0 -> x3, waiting for transfers between devices: none -> 3.96 us  [balance_page(): outcome_arr = lax.ppermute(outcome_arr, axis_name=shard_axis, perm=x_new)]
    dot_general x2, matrix products: 1.2 us -> 3.31 us  [body(): jnp.einsum('rs,rl->sl', half_weights, feats, preferred_element_type=jnp.f...]
  transfers between devices with their start and end apart: 0 -> 3, of which waited for: 0 -> 2; matrix products, arithmetic and copies ran while one was open for 0% -> 9% of each run, Pallas kernels for 0% -> 0%
where the time goes in v1:
time: 164 us; the launch traced here: 163 us
  blocking collectives  96.9 us (59%)
  matrix products  33.5 us (20%)
  other arithmetic  11.6 us (7%)
  local copies, waits for them, and re-layouts  8.91 us (5%)
  starting transfers between devices  6.71 us (4%)
  waiting for transfers between devices  3.96 us (2%)
    psum x2, blocking collectives, body(): numerator, total = lax.psum((numerator, total), ('pts', 'head'))  80.8 us
    dot_general x2, matrix products, body(): jnp.dot(upper, w_down[layer_index], preferred_element_type=jnp.float32)  8.53 us
    all_gather x1, blocking collectives, body(): full_in = lax.all_gather(w_in, 'head', axis=2, tiled=True)  8.24 us
    all_gather x1, blocking collectives, body(): full_fx = lax.all_gather(w_fx, 'head', axis=2, tiled=True)  7.81 us
    ppermute x3, starting transfers between devices, balance_page(): outcome_arr = lax.ppermute(outcome_arr, axis_name=shard_axis, perm=x_new)  6.71 us
    dot_general x2, matrix products, body(): projected = jnp.dot(half_weights, wide, preferred_element_type=jnp.float32)  6.26 us
    sub x2, matrix products, body(): weights = jax.nn.softmax(logits, axis=-1) * live[:, None, None]  5.24 us
    ppermute x3, waiting for transfers between devices, balance_page(): outcome_arr = lax.ppermute(outcome_arr, axis_name=shard_axis, perm=x_new)  3.96 us
  transfers between devices with their start and end apart: 3, of which 2 were waited for; matrix products, arithmetic and copies ran while one was open for 9% of the time, Pallas kernels for 0%

profile of v1, /device:TPU:0, one launch (start us, length us, event | category | flops | bytes accessed | tf_op | source)
XLA Modules:
  0.0 162.6 jit_solution(722386731942477610)
XLA Ops:
  0.0 3.0 %collective-permute-start = (bf16[2,32,128]{2,1,0:T(8,128)(2,1)}, bf16[2,32,128]{2,1,0:T(8,128)(2,1)}, u32[]{:S(2)}, u32[]{:S(2)}) collective-permute-start(bf16[2,32,128]{2,1,0:T(8,128)(2,1)} %param.28), channel_id=1, source_target_pairs={{0,1},{1,2},{2,3},{3,0},{4,5},{5,6},{6,7},{7,4},{8,9},{9,10},{10,1... | collective-permute-start | bytes 49160 | tf_op jit(solution)/shard_map/ppermute | solution.py:69
  3.0 0.6 fusion.102
  3.6 0.0 copy-start.13
  3.6 0.2 copy.26
  3.9 0.1 convert_reduce_fusion
  4.0 0.2 fusion.33
  4.2 0.1 copy-done.13
  4.3 0.1 copy.19
  4.4 0.1 copy.20
  4.5 0.1 copy-done.15
  4.5 0.2 broadcast_multiply_fusion
  4.7 0.1 mul.190
  4.8 8.2 %all_gather.6 = bf16[2,128,128]{1,2,0:T(8,128)(2,1)S(1)} all-gather(bf16[2,128,32]{1,2,0:T(8,128)(2,1)S(1)} %copy-done.11), channel_id=1, replica_groups=mesh['pts'=8,'head'=4] {'head'}, dimensions={2}, use_global_device_ids=true | all-gather | bytes 81920 | tf_op jit(solution)/shard_map/all_gather | solution.py:56
  13.1 0.6 slice_bitcast_fusion.33
  13.7 7.8 %all_gather.7 = bf16[2,128,128]{1,2,0:T(8,128)(2,1)S(1)} all-gather(bf16[2,128,32]{1,2,0:T(8,128)(2,1)S(1)} %copy-done.12), channel_id=1, replica_groups=mesh['pts'=8,'head'=4] {'head'}, dimensions={2}, use_global_device_ids=true | all-gather | bytes 81920 | tf_op jit(solution)/shard_map/all_gather | solution.py:57
  22.2 0.5 slice_bitcast_fusion.34
  22.7 1.2 convolution_convert_fusion.1
  24.0 1.8 %fusion.121 = (f32[2304,4]{0,1:T(4,128)S(1)}, f32[2304,4,32]{0,2,1:T(8,128)}) fusion(bf16[4,32,128]{2,1,0:T(8,128)(2,1)S(1)} %bitcast.210, f32[4]{0:T(128)S(1)} %get-tuple-element.28, bf16[2,128,128]{1,2,0:T(8,128)(2,1)S(1)} %all_gather.6, bf16[2304,128]{0,1:T(8,128)(2,1)S(1)} %copy.26, f32[128]{0:T(128)S(1)} %get-tuple-element.34, ...), kind=kOutput, calls=%fused_computation.184 | convolution fusion | flops 153944096 | bytes 1897984 | tf_op jit(solution)/shard_map/sub | solution.py:92
  25.8 1.6 fusion.57
  27.4 0.0 copy-done.2
  27.4 1.7 %fusion.39 = f32[4,32,4,32]{3,1,2,0:T(8,128)S(1)} fusion(bf16[4,32,2304,1]{2,1,0,3:T(8,128)(2,1)} %bitcast.213, f32[2304]{0:T(1024)S(1)} %fusion.83, f32[2304,4,32]{0,2,1:T(8,128)S(1)} %copy-done.2, f32[2304,4]{0,1:T(4,128)S(1)} %get-tuple-element.35), kind=kOutput, calls=%fused_computation.67 | convolution fusion | flops 76382208 | bytes 1881088 | tf_op jit(solution)/shard_map/rs,rl->sl/dot_general | solution.py:95
  29.2 40.2 %all-reduce.1 = (f32[4,32,32]{2,1,0:T(8,128)S(1)}, f32[4,32]{1,0:T(4,128)S(1)}) all-reduce(f32[4,32,32]{2,1,0:T(8,128)S(1)} %pad_maximum_fusion, f32[4,32]{1,0:T(4,128)S(1)} %fusion.57), channel_id=1, replica_groups=mesh['pts'=8,'head'=4] {'pts','head'}, use_global_device_ids=true, to_apply=%region_4.5 | all-reduce | flops 4224 | bytes 33792 | tf_op jit(solution)/shard_map/psum | solution.py:98
  69.4 0.9 fusion.92
  70.3 0.9 fusion.94
  71.3 0.9 fusion.90
  72.2 0.2 fusion.124
  72.5 0.3 convolution_convert_fusion.7
  72.8 2.3 %collective-permute-start.1 = (bf16[2,32,128]{2,1,0:T(8,128)(2,1)}, bf16[2,32,128]{2,1,0:T(8,128)(2,1)S(1)}, u32[]{:S(2)}, u32[]{:S(2)}) collective-permute-start(bf16[2,32,128]{2,1,0:T(8,128)(2,1)} %collective-permute-done), channel_id=1, source_target_pairs={{0,1},{1,2},{2,3},{3,0},{4,5},{5,6},{6,7},{7,4},{8,9},{9,10},{10,1... | collective-permute-start | bytes 49160 | tf_op jit(solution)/shard_map/ppermute | solution.py:69
  75.1 0.6 slice_bitcast_fusion.30
  75.7 2.0 %collective-permute-done.1 = bf16[2,32,128]{2,1,0:T(8,128)(2,1)S(1)} collective-permute-done((bf16[2,32,128]{2,1,0:T(8,128)(2,1)}, bf16[2,32,128]{2,1,0:T(8,128)(2,1)S(1)}, u32[]{:S(2)}, u32[]{:S(2)}) %collective-permute-start.1) | collective-permute-done | bytes 16416 | tf_op jit(solution)/shard_map/ppermute | solution.py:69
  77.7 1.4 collective-permute-start.2
  79.1 0.5 slice_bitcast_fusion.32
  79.6 0.7 mul.214
  80.4 2.0 %collective-permute-done.2 = bf16[2,32,128]{2,1,0:T(8,128)(2,1)S(1)} collective-permute-done((bf16[2,32,128]{2,1,0:T(8,128)(2,1)S(1)}, bf16[2,32,128]{2,1,0:T(8,128)(2,1)S(1)}, u32[]{:S(2)}, u32[]{:S(2)}) %collective-permute-start.2) | collective-permute-done | bytes 16416 | tf_op jit(solution)/shard_map/ppermute | solution.py:69
  82.4 0.7 constant_dynamic-update-slice_fusion.5
  83.1 0.7 constant_dynamic-update-slice_fusion.1
  83.9 0.6 constant_dynamic-slice_fusion.1
  84.5 2.8 %fusion.125 = (f32[2304]{0:T(1024)S(1)}, f32[2304,128]{0,1:T(8,128)}) fusion(f32[128]{0:T(128)S(1)} %get-tuple-element.26, bf16[4,32,32]{2,1,0:T(8,128)(2,1)S(1)} %convolution_convert_fusion.7, bf16[4,32,128]{2,1,0:T(8,128)(2,1)S(1)} %bitcast.212, f32[2304]{0:T(1024)S(1)} %fusion.83, f32[2304,4,32]{0,2,1:T(8,128)} %get-tuple-element.36, ...), kind=kOutput, calls=%fused_computation.186 | convolution fusion | flops 78624512 | bytes 3045888 | tf_op jit(solution)/shard_map/dot_general | solution.py:116
  87.3 1.4 multiply_reduce_fusion.2
  88.7 0.6 add_rsqrt_fusion.2
  89.3 4.6 %fusion.126 = (f32[2304]{0:T(1024)}, f32[2304,128]{0,1:T(8,128)S(1)}) fusion(f32[2304,128]{0,1:T(8,128)} %get-tuple-element.40, bf16[2,512,128]{2,1,0:T(8,128)(2,1)} %param.33, f32[128]{0:T(128)} %get-tuple-element.24, f32[128]{0:T(128)} %get-tuple-element.51, f32[2304]{0:T(1024)} %add_rsqrt_fusion.2, f32[2304]{0:T(1024)} %copy-done.9, ...), kind=kOutput, calls=%fused_computation.187 | convolution fusion | flops 617248512 | bytes 3835904 | tf_op jit(solution)/shard_map/dot_general | solution.py:125
  93.9 0.7 broadcast_multiply_fusion.3
  94.6 0.1 multiply_reduce_fusion.1
  94.8 0.4 add_convert_fusion.1
  95.2 0.8 copy-done.1
  96.0 1.1 convolution_convert_fusion
  97.1 3.4 %fusion.129 = (f32[2304,4]{0,1:T(4,128)}, f32[2304,4,32]{0,2,1:T(8,128)}) fusion(bf16[4,32,128]{2,1,0:T(8,128)(2,1)} %bitcast.209, bf16[2304,128]{0,1:T(8,128)(2,1)} %copy-done.1, f32[4]{0:T(128)S(1)} %copy-done.22, bf16[2,128,128]{1,2,0:T(8,128)(2,1)} %copy-done.7), kind=kOutput, calls=%fused_computation.188 | convolution fusion | flops 152174624 | bytes 1871888 | tf_op jit(solution)/shard_map/sub | solution.py:92
  100.5 1.6 fusion.59
  102.1 0.0 copy-done.3
  102.2 1.7 %fusion.37 = f32[4,32,4,32]{3,1,2,0:T(8,128)S(1)} fusion(bf16[4,32,2304,1]{2,1,0,3:T(8,128)(2,1)} %bitcast.208, f32[2304]{0:T(1024)S(1)} %fusion.83, f32[2304,4,32]{0,2,1:T(8,128)S(1)} %copy-done.3, f32[2304,4]{0,1:T(4,128)S(1)} %copy-done.10), kind=kOutput, calls=%fused_computation.65 | convolution fusion | flops 76382208 | bytes 1881088 | tf_op jit(solution)/shard_map/rs,rl->sl/dot_general | solution.py:95
  103.9 0.6 pad_maximum_fusion.1
  104.5 40.6 %all-reduce = (f32[4,32,32]{2,1,0:T(8,128)}, f32[4,32]{1,0:T(4,128)}) all-reduce(f32[4,32,32]{2,1,0:T(8,128)} %pad_maximum_fusion.1, f32[4,32]{1,0:T(4,128)S(1)} %fusion.59), channel_id=1, replica_groups=mesh['pts'=8,'head'=4] {'pts','head'}, use_global_device_ids=true, to_apply=%region_15.16 | all-reduce | flops 4224 | bytes 33792 | tf_op jit(solution)/shard_map/psum | solution.py:98
  145.1 0.7 broadcast_maximum_fusion
  145.8 1.1 fusion.86
  146.9 1.1 fusion.88
  147.9 1.1 fusion.84
  149.0 0.2 fusion.130
  149.3 0.9 convolution_convert_fusion.5
  150.2 3.4 %fusion.131 = (f32[2304]{0:T(1024)}, f32[2304,128]{0,1:T(8,128)}) fusion(f32[128]{0:T(128)} %get-tuple-element.25, f32[2304,128]{0,1:T(8,128)S(1)} %get-tuple-element.42, bf16[4,32,32]{2,1,0:T(8,128)(2,1)} %convolution_convert_fusion.5, bf16[4,32,128]{2,1,0:T(8,128)(2,1)} %bitcast.211, f32[2304]{0:T(1024)S(1)} %fusion.83, ...), kind=kOutput, calls=%fused_computation.190 | convolution fusion | flops 78329600 | bytes 3635712 | tf_op jit(solution)/shard_map/dot_general | solution.py:116
  153.7 0.8 broadcast_multiply_fusion.2
  154.5 1.4 multiply_reduce_fusion
  155.9 0.6 add_rsqrt_fusion
  156.5 4.0 %fusion.27 = bf16[2304,128]{0,1:T(8,128)(2,1)} fusion(f32[2304,128]{0,1:T(8,128)S(1)} %copy-done.4, f32[128]{0:T(128)S(1)} %copy-done.23, f32[128]{0:T(128)} %get-tuple-element.52, f32[2304]{0:T(1024)} %add_rsqrt_fusion, f32[2304]{0:T(1024)S(1)} %broadcast_multiply_fusion.2, bf16[2,512,128]{2,1,0:T(8,128)(2,1)} %param.33, bf16[2,128,512]{2,1,0:T(8,128)(2,1)} %param.32), kind=kOutput, calls=%fused_computation.35 | convolution fusion | flops 616660992 | bytes 3236864 | tf_op jit(solution)/shard_map/dot_general | solution.py:125
  160.5 2.1 %copy.22 = bf16[2304,128]{1,0:T(8,128)(2,1)} copy(bf16[2304,128]{0,1:T(8,128)(2,1)} %fusion.27) | data formatting | bytes 1179648 | tf_op jit(solution)/shard_map/convert_element_type | solution.py:126
  (62 shorter events, 0.3 us)
Async XLA Ops:
  0.0 3.5 %copy-start = (bf16[9216,128]{1,0:T(8,128)(2,1)S(1)}, bf16[9216,128]{1,0:T(8,128)(2,1)}, u32[]{:S(2)}) copy-start(bf16[9216,128]{1,0:T(8,128)(2,1)} %param.17) | copy-start | bytes 7077892
  0.0 72.8 %collective-permute-start = (bf16[2,32,128]{2,1,0:T(8,128)(2,1)}, bf16[2,32,128]{2,1,0:T(8,128)(2,1)}, u32[]{:S(2)}, u32[]{:S(2)}) collective-permute-start(bf16[2,32,128]{2,1,0:T(8,128)(2,1)} %param.28), channel_id=1, source_target_pairs={{0,1},{1,2},{2,3},{3,0},{4,5},{5,6},{6,7},{7,4},{8,9},{9,10},{10,1... | collective-permute-start | bytes 49160 | tf_op jit(solution)/shard_map/ppermute | solution.py:69
  3.6 0.7 copy-start.13
  3.8 0.7 copy-start.15
  3.9 1.0 copy-start.11
  3.9 9.2 %copy-start.16 = (f32[2,4]{1,0:T(2,128)S(1)}, f32[2,4]{1,0:T(2,128)}, u32[]{:S(2)}) copy-start(f32[2,4]{1,0:T(2,128)} %param.24) | copy-start | bytes 100
  3.9 9.8 %copy-start.12 = (bf16[2,128,32]{1,2,0:T(8,128)(2,1)S(1)}, bf16[2,128,32]{1,2,0:T(8,128)(2,1)}, u32[]{:S(2)}) copy-start(bf16[2,128,32]{1,2,0:T(8,128)(2,1)} %param.22) | copy-start | bytes 49156
  3.9 18.3 %copy-start.18 = (f32[2,128]{1,0:T(2,128)S(1)}, f32[2,128]{1,0:T(2,128)}, u32[]{:S(2)}) copy-start(f32[2,128]{1,0:T(2,128)} %param.20) | copy-start | bytes 3076
  3.9 18.3 %copy-start.19 = (f32[2,128]{1,0:T(2,128)S(1)}, f32[2,128]{1,0:T(2,128)}, u32[]{:S(2)}) copy-start(f32[2,128]{1,0:T(2,128)} %param.19) | copy-start | bytes 3076
  13.1 12.7 %copy-start.7 = (bf16[2,128,128]{1,2,0:T(8,128)(2,1)}, bf16[2,128,128]{1,2,0:T(8,128)(2,1)S(1)}, u32[]{:S(2)}) copy-start(bf16[2,128,128]{1,2,0:T(8,128)(2,1)S(1)} %all_gather.6) | copy-start | bytes 196612
  21.5 1.2 copy-start.5
  25.8 1.6 %copy-start.2 = (f32[2304,4,32]{0,2,1:T(8,128)S(1)}, f32[2304,4,32]{0,2,1:T(8,128)}, u32[]{:S(2)}) copy-start(f32[2304,4,32]{0,2,1:T(8,128)} %get-tuple-element.36) | copy-start | bytes 3538948
  29.1 50.1 %copy-start.17 = (f32[2,128]{1,0:T(2,128)S(1)}, f32[2,128]{1,0:T(2,128)}, u32[]{:S(2)}) copy-start(f32[2,128]{1,0:T(2,128)} %param.29) | copy-start | bytes 3076
  29.1 54.0 %copy-start.8 = (bf16[2,32,128]{2,1,0:T(8,128)(2,1)S(1)}, bf16[2,32,128]{2,1,0:T(8,128)(2,1)}, u32[]{:S(2)}) copy-start(bf16[2,32,128]{2,1,0:T(8,128)(2,1)} %param.28) | copy-start | bytes 49156
  29.1 46.0 %copy-start.20 = (f32[2,128]{1,0:T(2,128)S(1)}, f32[2,128]{1,0:T(2,128)}, u32[]{:S(2)}) copy-start(f32[2,128]{1,0:T(2,128)} %param.31) | copy-start | bytes 3076
  29.1 46.0 %copy-start.21 = (f32[2,128]{1,0:T(2,128)S(1)}, f32[2,128]{1,0:T(2,128)}, u32[]{:S(2)}) copy-start(f32[2,128]{1,0:T(2,128)} %param.30) | copy-start | bytes 3076
  72.8 4.9 %collective-permute-start.1 = (bf16[2,32,128]{2,1,0:T(8,128)(2,1)}, bf16[2,32,128]{2,1,0:T(8,128)(2,1)S(1)}, u32[]{:S(2)}, u32[]{:S(2)}) collective-permute-start(bf16[2,32,128]{2,1,0:T(8,128)(2,1)} %collective-permute-done), channel_id=1, source_target_pairs={{0,1},{1,2},{2,3},{3,0},{4,5},{5,6},{6,7},{7,4},{8,9},{9,10},{10,1... | collective-permute-start | bytes 49160 | tf_op jit(solution)/shard_map/ppermute | solution.py:69
  77.7 4.6 %collective-permute-start.2 = (bf16[2,32,128]{2,1,0:T(8,128)(2,1)S(1)}, bf16[2,32,128]{2,1,0:T(8,128)(2,1)S(1)}, u32[]{:S(2)}, u32[]{:S(2)}) collective-permute-start(bf16[2,32,128]{2,1,0:T(8,128)(2,1)S(1)} %collective-permute-done.1), channel_id=1, source_target_pairs={{0,1},{1,2},{2,3},{3,0},{4,5},{5,6},{6,7},{7,4},{8,9},{9,10},{10,1... | collective-permute-start | bytes 49160 | tf_op jit(solution)/shard_map/ppermute | solution.py:69
  87.3 2.0 %copy-start.9 = (f32[2304]{0:T(1024)}, f32[2304]{0:T(1024)S(1)}, u32[]{:S(2)}) copy-start(f32[2304]{0:T(1024)S(1)} %broadcast_multiply_fusion.4) | copy-start | bytes 27652
  93.9 0.9 copy-start.14
  94.7 1.3 copy-start.6
  95.1 0.8 copy-start.1
  96.0 1.1 copy-start.22
  100.5 1.6 %copy-start.3 = (f32[2304,4,32]{0,2,1:T(8,128)S(1)}, f32[2304,4,32]{0,2,1:T(8,128)}, u32[]{:S(2)}) copy-start(f32[2304,4,32]{0,2,1:T(8,128)} %get-tuple-element.44) | copy-start | bytes 3538948
  100.5 1.6 %copy-start.10 = (f32[2304,4]{0,1:T(4,128)S(1)}, f32[2304,4]{0,1:T(4,128)}, u32[]{:S(2)}) copy-start(f32[2304,4]{0,1:T(4,128)} %get-tuple-element.43) | copy-start | bytes 110596
  153.7 2.8 %copy-start.4 = (f32[2304,128]{0,1:T(8,128)S(1)}, f32[2304,128]{0,1:T(8,128)}, u32[]{:S(2)}) copy-start(f32[2304,128]{0,1:T(8,128)} %get-tuple-element.48) | copy-start | bytes 3538948
  153.7 2.8 %copy-start.23 = (f32[128]{0:T(128)S(1)}, f32[128]{0:T(128)}, u32[]{:S(2)}) copy-start(f32[128]{0:T(128)} %get-tuple-element.23) | copy-start | bytes 1540
